TPU v7x, 256 devices: a whole 4x4x8 slice. The times are simulated.
256 devices in a mesh: section: 2 (over y_hi), dp: 16 (over z, core), vocab: 8 (over y_lo, x).
Axes of the slice: x: 4, y: 4 (y_hi: 2, y_lo: 2; y = y_hi * 2 + y_lo), z: 8, core: 2. Of those that a mesh axis runs over, the one named last changes fastest.
Arguments:
- activations: bfloat16 [2, 2048, 2048], P('section', 'dp'), may hold values from -32 to 32
- token_ids: int32 [2, 2048], replicated, may hold values from 0 to 65535
- embed_table: bfloat16 [65536, 2048], P(('dp', 'vocab')), may hold values from -3 to 3
Outputs:
- tied_grad: bfloat16 [128, 2, 256, 2048], P(('dp', 'vocab'), 'section')
All inputs are finite; a program needn't handle non-finite values.
Results may differ from a plain program's by a relative error of at most 0.0029.
Values may be sent and summed in bfloat16 or wider, within the bound.
A program may use at most 128 MiB of HBM per device.

v0:
```python
import jax
import jax.numpy as jnp
from jax import lax
from jax.sharding import Mesh
from jax.sharding import PartitionSpec as P

DP = ("dp_0", "dp_1")
VOCAB = ("vocab_0", "vocab_1")
SECTION_DP_VOCAB = ("section", "dp_0", "dp_1", "vocab_0", "vocab_1")
DP_VOCAB = ("dp_0", "dp_1", "vocab_0", "vocab_1")


def from_partner(block, axis, apart):
    count = lax.axis_size(axis)
    route = []
    for low in range(count):
        high = low | 1 << apart
        if high != low and high < count:
            route += [(low, high), (high, low)]
    return lax.ppermute(block, axis, route)


def collected_together(shard, axis):
    leaves = jax.tree.leaves(shard)
    sequence = sorted(range(len(leaves)), key=lambda k: -leaves[k].size)
    width = (1, *leaves[sequence[0]].shape)[-1]
    lines = [
        jnp.pad(leaves[k].reshape(-1), (0, -leaves[k].size % width)).reshape(-1, width)
        for k in sequence
    ]
    both, at, found = (lax.all_gather(jnp.concatenate(lines), axis), 0, {})
    for k, line in zip(sequence, lines):
        share = both[:, at : at + len(line)].reshape(len(both), -1)
        found[k] = share[:, : leaves[k].size].reshape(-1, *leaves[k].shape)
        at += len(line)
    numbers = iter(range(len(leaves)))
    return jax.tree.map(lambda _: found[next(numbers)], shard)


def combined_by_axis(shard, axes, combine):
    for axis in axes:
        pieces = collected_together(shard, axis)
        shard = jax.tree.map(lambda part: part[0], pieces)
        for k in range(1, lax.axis_size(axis)):
            shard = combine(shard, jax.tree.map(lambda part: part[k], pieces))
    return shard


def combine(left_pair, right_pair):
    row_peak = jnp.maximum(left_pair[0], right_pair[0])
    row_total = left_pair[1] * jnp.exp(left_pair[0] - row_peak) + right_pair[1] * jnp.exp(
        right_pair[0] - row_peak
    )
    return (row_peak, row_total)


def spread_rows(row_tuple):
    return (
        lax.all_gather(row_tuple[0], DP, axis=0, tiled=True),
        lax.all_gather(row_tuple[1], DP, axis=0, tiled=True),
    )


def local_stats(logits):
    row_peak = jnp.max(logits, axis=1)
    row_total = jnp.sum(jnp.exp(logits - row_peak[:, None]), axis=1)
    return (row_peak, row_total)


def body(activations, token_ids, embed_table):
    own_rows = activations[0]
    model_width = own_rows.shape[1]
    table_count = embed_table.shape[0]
    section_index = lax.axis_index("section")
    half_rows = table_count // lax.axis_size("section")
    block_first = (lax.axis_index(DP) * lax.axis_size(VOCAB) + lax.axis_index(VOCAB)) * table_count
    partner = from_partner(own_rows, "section", 0)
    cot_rows = jnp.where(section_index == 0, own_rows, partner)
    hid_rows = jnp.where(section_index == 0, partner, own_rows)
    cot_all, hid_all = spread_rows((cot_rows, hid_rows))
    my_table = lax.dynamic_slice_in_dim(embed_table, section_index * half_rows, half_rows, 0)
    row_first = block_first + section_index * half_rows
    positions = jnp.arange(half_rows, dtype=jnp.int32)[None, :]
    target_hot = (token_ids[1] - row_first)[:, None] == positions
    input_hot = (token_ids[0] - row_first)[:, None] == positions
    logits = lax.dot_general(
        hid_all, my_table, (((1,), (1,)), ((), ())), preferred_element_type=jnp.float32
    )
    row_peak, row_total = local_stats(logits)
    peak_all, total_all = combined_by_axis((row_peak, row_total), SECTION_DP_VOCAB, combine)
    probs = jnp.exp(logits - peak_all[:, None]) / total_all[:, None]
    last_part = (probs - target_hot.astype(jnp.float32)).astype(jnp.bfloat16)
    first_part = input_hot.astype(jnp.bfloat16)
    summed = lax.dot_general(
        last_part, hid_all, (((0,), (0,)), ((), ())), preferred_element_type=jnp.float32
    )
    summed = summed + lax.dot_general(
        first_part, cot_all, (((0,), (0,)), ((), ())), preferred_element_type=jnp.float32
    )
    return summed.astype(jnp.bfloat16).reshape(1, 1, half_rows, model_width)


def solution(mesh):
    finer = Mesh(
        mesh.devices.reshape(mesh.shape["section"], 8, 2, 2, 4),
        ("section", "dp_0", "dp_1", "vocab_0", "vocab_1"),
    )
    in_specs = (P("section", DP, None), P(), P(DP_VOCAB, None))
    out_specs = P(DP_VOCAB, "section", None, None)
    return jax.shard_map(body, mesh=finer, in_specs=in_specs, out_specs=out_specs, check_vma=False)
```

profile of v0, /device:TPU:1, one launch (start us, length us, event | category | flops | bytes accessed | tf_op | source)
XLA Modules:
  0.0 161.4 jit_solution(14041888525596776392)
XLA Ops:
  6.5 0.0 copy-start
  6.5 0.0 all-gather.13.cloned.1.call-start
  6.5 3.7 %collective-permute-start = (bf16[128,2048]{1,0:T(8,128)(2,1)}, bf16[128,2048]{1,0:T(8,128)(2,1)S(1)}, u32[]{:S(2)}, u32[]{:S(2)}) collective-permute-start(bf16[128,2048]{1,0:T(8,128)(2,1)} %bitcast.264), channel_id=1, source_target_pairs={{0,128},{128,0},{1,129},{129,1},{2,130},{130,2},{3,131},{131,3},{4... | collective-permute-start | bytes 1572872 | tf_op jit(solution)/shard_map/ppermute | solution.py:20
  10.3 10.9 %collective-permute-done = bf16[128,2048]{1,0:T(8,128)(2,1)S(1)} collective-permute-done((bf16[128,2048]{1,0:T(8,128)(2,1)}, bf16[128,2048]{1,0:T(8,128)(2,1)S(1)}, u32[]{:S(2)}, u32[]{:S(2)}) %collective-permute-start) | collective-permute-done | bytes 524320 | tf_op jit(solution)/shard_map/ppermute | solution.py:20
  21.2 2.1 %broadcast_select_fusion.1 = (bf16[128,2048]{1,0:T(8,128)(2,1)}, bf16[128,2048]{1,0:T(8,128)(2,1)}) fusion(bf16[128,2048]{1,0:T(8,128)(2,1)S(1)} %collective-permute-done, pred[]{:T(512)S(6)} %eq.14, bf16[1,128,2048]{2,1,0:T(8,128)(2,1)} %param.3), kind=kLoop, calls=%fused_computation.15 | loop fusion | flops 524288 | bytes 2097153 | tf_op jit(solution)/shard_map/jit(_where)/select_n | solution.py:79
  23.3 0.0 all-gather.13.cloned.1.call-update
  23.3 0.0 all-gather.15.cloned.1.call-start
  23.4 0.7 all-gather.15.cloned.1.call-update
  24.1 0.0 copy-done.3
  24.1 60.1 %all-gather.13.cloned.1.call-done = bf16[2048,2048]{1,0:T(8,128)(2,1)} async-done(((bf16[128,2048]{1,0:T(8,128)(2,1)}), bf16[2048,2048]{1,0:T(8,128)(2,1)}) %all-gather.13.cloned.1.call-update) | async-done | bytes 8388624 | tf_op jit(solution)/shard_map/all_gather | solution.py:60
  84.2 0.0 copy-done
  84.2 5.8 %fusion.56 = (f32[2048]{0:T(1024)S(1)}, f32[2048,256]{0,1:T(8,128)S(1)}) fusion(bf16[2048,2048]{1,0:T(8,128)(2,1)} %all-gather.13.cloned.1.call-done, bf16[512,2048]{1,0:T(8,128)(2,1)S(1)} %copy-done, s32[]{:T(128)S(6)} %select_n.17), kind=kOutput, calls=%fused_computation.95 | convolution fusion | flops 2148005888 | bytes 11542532 | tf_op jit(solution)/shard_map/dot_general | solution.py:86
  90.0 1.3 copy-done.1
  91.3 0.3 exponential_reduce_fusion
  91.7 4.8 %all-gather.5 = f32[2,2,2048]{2,1,0:T(2,128)S(1)} all-gather(f32[1,2,2048]{2,1,0:T(2,128)S(1)} %maximum_bitcast_fusion), channel_id=2, replica_groups=mesh['section'=2,'dp_0'=8,'dp_1'=2,'vocab_0'=2,'vocab_1'=4] {'section'}, dimensions={0}, use_global_device_ids=true | all-gather | bytes 49152 | tf_op jit(solution)/shard_map/all_gather | solution.py:31
  96.5 21.3 %all-gather.6 = f32[8,2,2048]{2,1,0:T(2,128)S(1)} all-gather(f32[1,2,2048]{2,1,0:T(2,128)S(1)} %maximum_bitcast_fusion.1), channel_id=3, replica_groups=mesh['section'=2,'dp_0'=8,'dp_1'=2,'vocab_0'=2,'vocab_1'=4] {'dp_0'}, dimensions={0}, use_global_device_ids=true | all-gather | bytes 147456 | tf_op jit(solution)/shard_map/all_gather | solution.py:31
  117.8 0.2 fusion.16
  118.0 6.9 %all-gather.7 = f32[2,2,2048]{2,1,0:T(2,128)S(1)} all-gather(f32[1,2,2048]{2,1,0:T(2,128)S(1)} %maximum_bitcast_fusion.2), channel_id=4, replica_groups=mesh['section'=2,'dp_0'=8,'dp_1'=2,'vocab_0'=2,'vocab_1'=4] {'dp_1'}, dimensions={0}, use_global_device_ids=true | all-gather | bytes 49152 | tf_op jit(solution)/shard_map/all_gather | solution.py:31
  125.0 3.7 %all-gather.8 = f32[2,2,2048]{2,1,0:T(2,128)S(1)} all-gather(f32[1,2,2048]{2,1,0:T(2,128)S(1)} %maximum_bitcast_fusion.3), channel_id=5, replica_groups=mesh['section'=2,'dp_0'=8,'dp_1'=2,'vocab_0'=2,'vocab_1'=4] {'vocab_0'}, dimensions={0}, use_global_device_ids=true | all-gather | bytes 49152 | tf_op jit(solution)/shard_map/all_gather | solution.py:31
  128.7 10.5 %all-gather.9 = f32[4,2,2048]{2,1,0:T(2,128)S(1)} all-gather(f32[1,2,2048]{2,1,0:T(2,128)S(1)} %maximum_bitcast_fusion.4), channel_id=6, replica_groups=mesh['section'=2,'dp_0'=8,'dp_1'=2,'vocab_0'=2,'vocab_1'=4] {'vocab_1'}, dimensions={0}, use_global_device_ids=true | all-gather | bytes 81920 | tf_op jit(solution)/shard_map/all_gather | solution.py:31
  139.2 0.1 fusion.55
  139.3 2.5 %all-gather.15.cloned.1.call-done = bf16[2048,2048]{1,0:T(8,128)(2,1)} async-done(((bf16[128,2048]{1,0:T(8,128)(2,1)}), bf16[2048,2048]{1,0:T(8,128)(2,1)}) %all-gather.15.cloned.1.call-update) | async-done | bytes 8388624 | tf_op jit(solution)/shard_map/all_gather | solution.py:59
  141.7 6.0 %fusion.2 = f32[256,2048]{1,0:T(8,128)S(1)} fusion(bf16[2048,2048]{1,0:T(8,128)(2,1)} %all-gather.15.cloned.1.call-done, s32[2048]{0:T(1024)S(1)} %bitcast.279), kind=kOutput, calls=%fused_computation.7 | convolution fusion | flops 2148007936 | bytes 10493952 | tf_op jit(solution)/shard_map/dot_general | solution.py:97
  147.7 6.9 %fusion.1 = bf16[1,1,256,2048]{3,2,1,0:T(8,128)(2,1)} fusion(f32[256,2048]{1,0:T(8,128)S(1)} %fusion.2, bf16[2048,2048]{1,0:T(8,128)(2,1)} %all-gather.13.cloned.1.call-done, f32[2048,256]{0,1:T(8,128)S(1)} %copy-done.2, s32[2048]{0:T(1024)S(1)} %bitcast.278, f32[2048]{0:T(1024)S(1)} %get-tuple-element.5, f32[2048]{0:T(1024)S(1)} %get-tuple-element.6), kind=kOutput, calls=%fused_computation.2 | convolution fusion | flops 2151677952 | bytes 13656064 | tf_op jit(solution)/shard_map/dot_general | solution.py:94
  (15 shorter events, 0.3 us)
Async XLA Ops:
  6.5 77.7 %copy-start = (bf16[512,2048]{1,0:T(8,128)(2,1)S(1)}, bf16[512,2048]{1,0:T(8,128)(2,1)}, u32[]{:S(2)}) copy-start(bf16[512,2048]{1,0:T(8,128)(2,1)} %param.5) | copy-start | bytes 6291460
  6.5 17.5 %copy-start.3 = (s32[2,2048]{1,0:T(2,128)S(1)}, s32[2,2048]{1,0:T(2,128)}, u32[]{:S(2)}) copy-start(s32[2,2048]{1,0:T(2,128)} %param.4) | copy-start | bytes 49156
  6.5 77.7 %all-gather.13.cloned.1.call-start = ((), (), s32[]{:S(2)}) async-start(), calls=%async_computation | async-start | bytes 8912896 | tf_op jit(solution)/shard_map/all_gather | solution.py:60
  6.5 14.7 %collective-permute-start = (bf16[128,2048]{1,0:T(8,128)(2,1)}, bf16[128,2048]{1,0:T(8,128)(2,1)S(1)}, u32[]{:S(2)}, u32[]{:S(2)}) collective-permute-start(bf16[128,2048]{1,0:T(8,128)(2,1)} %bitcast.264), channel_id=1, source_target_pairs={{0,128},{128,0},{1,129},{129,1},{2,130},{130,2},{3,131},{131,3},{4... | collective-permute-start | bytes 1572872 | tf_op jit(solution)/shard_map/ppermute | solution.py:20
  23.3 118.4 %all-gather.15.cloned.1.call-start = ((), (), s32[]{:S(2)}) async-start(), calls=%async_computation.1 | async-start | bytes 8912896 | tf_op jit(solution)/shard_map/all_gather | solution.py:59
  90.0 1.3 copy-start.1
  141.7 6.0 %copy-start.2 = (f32[2048,256]{0,1:T(8,128)S(1)}, f32[2048,256]{0,1:T(8,128)}, u32[]{:S(2)}) copy-start(f32[2048,256]{0,1:T(8,128)} %copy-done.1) | copy-start | bytes 6291460
Sparse Core Ops, SparseCore 0:
  23.4 60.7 all-gather.12
  86.1 55.6 all-gather.14
where the time goes:
time: 162 us; the launch traced here: 161 us
  waiting for transfers between devices  74.2 us (46%)
  blocking collectives  47.1 us (29%)
  matrix products  18.6 us (11%)
  between operations  13.5 us (8%)
  starting transfers between devices  3.78 us (2%)
  other arithmetic  2.85 us (2%)
    all_gather x1, waiting for transfers between devices, spread_rows(): lax.all_gather(row_tuple[1], DP, axis=0, tiled=True)  60.1 us
    all_gather x5, blocking collectives, collected_together(): both, at, found = (lax.all_gather(jnp.concatenate(lines), axis), 0, {})  47.1 us
    ppermute x1, waiting for transfers between devices, from_partner(): return lax.ppermute(block, axis, route)  10.9 us
    dot_general x1, matrix products, body(): lax.dot_general(last_part, hid_all, (((0,), (0,)), ((), ())), preferred_e...  6.89 us
    dot_general x1, matrix products, body(): lax.dot_general(first_part, cot_all, (((0,), (0,)), ((), ())), preferred_...  5.97 us
    dot_general x1, matrix products, body(): lax.dot_general(hid_all, my_table, (((1,), (1,)), ((), ())), preferred_el...  5.75 us
    ppermute x1, starting transfers between devices, from_partner(): return lax.ppermute(block, axis, route)  3.73 us
  transfers between devices with their start and end apart: 3, of which 3 were waited for; matrix products, arithmetic and copies ran while one was open for 4% of the time, Pallas kernels for 0%

commit v1 on v0

v1 whole, which is shorter than its diff:
```python
import jax
import jax.numpy as jnp
from jax import lax
from jax.experimental import pallas as pl
from jax.experimental.pallas import tpu as pltpu
from jax.sharding import PartitionSpec as P

MESH = pl.DeviceIdType.MESH
COT, HID = 0, 1
Z, X, Y = 8, 4, 4
SLOTS = ((0, 1), (1, 2), (3, 2), (5, 2), (7, 1))
WIDTH = 2048
CUT_X, CUT_Y = 1024, 1664
COLUMNS = ((0, CUT_X), (CUT_X, CUT_Y - CUT_X), (CUT_Y, WIDTH - CUT_Y))
ROWS = 256
DOT = dict(preferred_element_type=jnp.float32)


def merge(pairs):
    peak = pairs[0][0]
    for other, _ in pairs[1:]:
        peak = jnp.maximum(peak, other)
    total = pairs[0][1] * jnp.exp(pairs[0][0] - peak)
    for other, part in pairs[1:]:
        total = total + part * jnp.exp(other - peak)
    return peak, total


def kernel(
    act, ids, table, out,
    buf, tab, scores, last_w, first_w, acc, out_v,
    own_stat, core_stat, sent_stat, x_stat, y_stat, z_stat, fin_stat,
    local_sem, boot_s, boot_r, z_s, z_r, ring_s, ring_r, core_s, core_r, stat_s, stat_r,
):
    s = lax.axis_index("section")
    d = lax.axis_index("dp")
    v = lax.axis_index("vocab")
    z, c = lax.div(d, 2), lax.rem(d, 2)
    yl, x = lax.div(v, 4), lax.rem(v, 4)
    y = 2 * s + yl
    row_first = (d * 8 + v) * 512 + s * ROWS

    def z_dev(k):
        return {"dp": lax.rem(z + k + Z, Z) * 2 + c}

    def x_dev(k):
        return {"vocab": yl * 4 + lax.rem(x + k + X, X)}

    def y_dev(k):
        to = lax.rem(y + k + Y, Y)
        return {"section": lax.div(to, 2), "vocab": lax.rem(to, 2) * 4 + x}

    core_dev = {"dp": z * 2 + 1 - c}
    cross_dev = {"section": 1 - s, "vocab": (1 - yl) * 4 + x}

    def remote(src, dst, send, recv, device):
        return pltpu.make_async_remote_copy(
            src_ref=src, dst_ref=dst, send_sem=send, recv_sem=recv,
            device_id=device, device_id_type=MESH,
        )

    load_own = pltpu.make_async_copy(act, buf.at[s, 0, c], local_sem.at[0])
    load_own.start()
    load_table = pltpu.make_async_copy(table.at[pl.ds(s * ROWS, ROWS)], tab, local_sem.at[1])
    load_table.start()

    barrier = pltpu.get_barrier_semaphore()
    peers = [z_dev(k) for k in range(1, Z)] + [x_dev(k) for k in range(1, X)]
    peers += [y_dev(k) for k in range(1, Y)] + [core_dev]
    for peer in peers:
        pl.semaphore_signal(barrier, inc=1, device_id=peer, device_id_type=MESH)

    def region(array, slot, count, part, tile, tiles):
        first, width = COLUMNS[part]
        return buf.at[array, pl.ds(slot, count), c, pl.ds(tile, tiles), :, pl.ds(first, width)]

    def boot_copy(k):
        far_y = 3 - y
        if k == 0:
            ref = region(s, 0, 1, 0, 2 * x, 2)
        elif k == 1:
            ref = region(s, 0, 1, 1, 2 * far_y, 2)
        elif k == 2:
            ref = region(s, 0, 1, 2, 0, 8)
        elif k < 6:
            ref = region(s, 0, 1, 0, 2 * lax.rem(x + k - 2, X), 2)
        else:
            ref = region(s, 0, 1, 1, 2 * lax.rem(far_y + k - 5, Y), 2)
        return remote(ref, ref, boot_s.at[k], boot_r.at[k], cross_dev)

    def z_copy(array, way, t, part):
        slot = 0 if t == 0 else 2 * t - 1 + way
        to = 2 * t + 1 + way if t < 3 else 7
        quarter = 2 * (x, y, 0)[part]
        tiles = (2, 2, 8)[part]
        if t == 3:
            tiles = tiles // 2
            quarter = quarter + way * tiles
        return remote(
            region(array, slot, 1, part, quarter, tiles),
            region(array, to, 1, part, quarter, tiles),
            z_s.at[array, way, t, part], z_r.at[array, way, t, part],
            z_dev(1 if way == 0 else -1),
        )

    def ring_copy(array, dim, t, k):
        slot, count = SLOTS[t]
        q, dev = ((x, x_dev), (y, y_dev))[dim]
        if k < 2:
            tile, tiles = 2 * q, 2
        elif k == 2:
            tile, tiles = 2 * lax.rem(q + 3, 4), 1
        else:
            tile, tiles = 2 * lax.rem(q + 1, 4) + 1, 1
        ref = region(array, slot, count, dim, tile, tiles)
        return remote(
            ref, ref, ring_s.at[array, dim, t - 1, k], ring_r.at[array, dim, t - 1, k],
            dev(1 if k % 2 == 0 else -1),
        )

    def core_copy(array, t):
        slot, count = SLOTS[t]
        ref = buf.at[array, pl.ds(slot, count), c]
        return remote(ref, ref, core_s.at[array, t], core_r.at[array, t], core_dev)

    def start(array):
        for part in range(3):
            @pl.when(s != array)
            def _():
                boot_copy(part).wait_recv()

            for way in range(2):
                z_copy(array, way, 0, part).start()

    def step_quarters(array, t):
        for part in range(2):
            for way in range(2):
                z_copy(array, way, t - 1, part).wait_recv()
                if t < 4:
                    z_copy(array, way, t, part).start()
            for k in range(2):
                ring_copy(array, part, t, k).start()

    def step_whole(array, t):
        for way in range(2):
            z_copy(array, way, t - 1, 2).wait_recv()
            if t < 4:
                z_copy(array, way, t, 2).start()

    def pass_on(array, t):
        for dim in range(2):
            for k in range(2):
                ring_copy(array, dim, t, k).wait_recv()
                ring_copy(array, dim, t, k + 2).start()

    def share(array, t):
        for dim in range(2):
            for k in range(2):
                ring_copy(array, dim, t, k + 2).wait_recv()
        core_copy(array, t).start()

    def chip_of(slot):
        half = lax.div(slot + 1, 2)
        return lax.rem(z + jnp.where(lax.rem(slot, 2) == 1, Z - half, half), Z)

    def score(t):
        core_copy(HID, t).wait_recv()
        first, count = SLOTS[t]

        def one(slot, carry):
            rows = buf[HID, slot].reshape(256, WIDTH)
            block = lax.dot_general(tab[...], rows, (((1,), (1,)), ((), ())), **DOT)
            scores[slot] = block
            peak = jnp.max(block, axis=0, keepdims=True)
            total = jnp.sum(jnp.exp(block - peak), axis=0, keepdims=True)
            chip = chip_of(slot)
            for core in range(2):
                lanes = slice(core * 128, core * 128 + 128)
                own_stat[core, 0, pl.ds(chip, 1), :] = peak[:, lanes]
                own_stat[core, 1, pl.ds(chip, 1), :] = total[:, lanes]
            return carry

        lax.fori_loop(first, first + count, one, 0)

    def add_first(first, count, finish):
        def one(n, carry):
            cols = pl.ds(pl.multiple_of(n * 256, 256), 256)
            rows = buf[COT, pl.ds(first, count), :, :, :, cols].reshape(count * 256, 256)
            part = jnp.dot(first_w[:, first * 256 : (first + count) * 256], rows, **DOT)
            total = acc[:, cols] + part
            if finish:
                out_v[:, cols] = total.astype(jnp.bfloat16)
                pltpu.make_async_copy(
                    out_v.at[:, cols], out.at[:, cols], local_sem.at[2 + n]
                ).start()
            else:
                acc[:, cols] = total
            return carry

        lax.fori_loop(0, WIDTH // 256, one, 0)

    def hot(index, slot, core):
        at = pl.multiple_of(chip_of(slot) * 256 + core * 128, 128)
        wanted = ids[pl.ds(index, 1), pl.ds(at, 128)] - row_first
        return lax.broadcasted_iota(jnp.int32, (ROWS, 128), 0) == wanted

    def lanes_of(slot, core):
        return pl.ds(pl.multiple_of(slot * 256 + core * 128, 128), 128)

    def stat_core(k):
        if k == 0:
            return remote(own_stat.at[1 - c], core_stat, stat_s.at[0], stat_r.at[0], core_dev)
        return remote(sent_stat.at[3], fin_stat.at[c], stat_s.at[1], stat_r.at[1], core_dev)

    def stat_axis(axis, k):
        into, dev, at = ((x_stat, x_dev, 2), (y_stat, y_dev, 5), (z_stat, z_dev, 8))[axis]
        at = at + k - 1
        return remote(sent_stat.at[axis], into.at[k - 1], stat_s.at[at], stat_r.at[at], dev(k))

    counts = (X, Y, Z)

    def stat_send(axis, pairs):
        peak, total = merge(pairs)
        sent_stat[axis, 0] = peak
        sent_stat[axis, 1] = total
        if axis < 3:
            for k in range(1, counts[axis]):
                stat_axis(axis, k).start()

    def stat_take(axis):
        into = (x_stat, y_stat, z_stat)[axis]
        pairs = [(sent_stat[axis, 0], sent_stat[axis, 1])]
        for k in range(1, counts[axis]):
            stat_axis(axis, k).wait_recv()
            pairs.append((into[k - 1, 0], into[k - 1, 1]))
        return pairs

    load_own.wait()
    pl.semaphore_wait(barrier, len(peers))

    for k in range(3):
        boot_copy(k).start()
    start(HID)
    for k in range(3, 9):
        boot_copy(k).start()

    @pl.when(s == HID)
    def _():
        core_copy(HID, 0).start()

    @pl.when(s == COT)
    def _():
        core_copy(COT, 0).start()

    def first_rows(slot, carry):
        for core in range(2):
            first_w[:, lanes_of(slot, core)] = hot(0, slot, core).astype(jnp.bfloat16)
        return carry

    lax.fori_loop(0, 8, first_rows, 0)
    load_table.wait()

    step_quarters(HID, 1)
    step_whole(HID, 1)

    @pl.when(s == COT)
    def _():
        for k in range(3, 9):
            boot_copy(k).wait_recv()
        core_copy(HID, 0).start()

    step_quarters(HID, 2)
    pass_on(HID, 1)
    step_whole(HID, 2)
    step_quarters(HID, 3)
    pass_on(HID, 2)
    step_whole(HID, 3)
    share(HID, 1)
    score(0)
    start(COT)

    @pl.when(s == HID)
    def _():
        for k in range(3, 9):
            boot_copy(k).wait_recv()
        core_copy(COT, 0).start()

    step_quarters(HID, 4)
    pass_on(HID, 3)
    step_whole(HID, 4)
    share(HID, 2)
    score(1)
    pass_on(HID, 4)
    share(HID, 3)
    score(2)
    step_quarters(COT, 1)
    step_whole(COT, 1)
    share(HID, 4)
    score(3)
    score(4)
    stat_core(0).start()
    step_quarters(COT, 2)
    pass_on(COT, 1)
    stat_core(0).wait_recv()
    mine = own_stat[pl.ds(c, 1)]
    stat_send(0, [(mine[0, 0], mine[0, 1]), (core_stat[0], core_stat[1])])
    step_whole(COT, 2)
    stat_send(1, stat_take(0))
    step_quarters(COT, 3)
    pass_on(COT, 2)
    stat_send(2, stat_take(1))
    step_whole(COT, 3)
    share(COT, 1)
    stat_send(3, stat_take(2))
    stat_core(1).start()
    fin_stat[pl.ds(c, 1)] = sent_stat[pl.ds(3, 1)]
    step_quarters(COT, 4)
    pass_on(COT, 3)
    step_whole(COT, 4)
    share(COT, 2)
    pass_on(COT, 4)
    stat_core(1).wait_recv()

    def last_rows(slot, carry):
        chip = chip_of(slot)
        for core in range(2):
            peak = fin_stat[core, 0, pl.ds(chip, 1), :]
            total = fin_stat[core, 1, pl.ds(chip, 1), :]
            lanes = slice(core * 128, core * 128 + 128)
            probs = jnp.exp(scores[slot, :, lanes] - peak) / total
            weight = probs - jnp.where(hot(1, slot, core), 1.0, 0.0)
            last_w[:, lanes_of(slot, core)] = weight.astype(jnp.bfloat16)
        return carry

    lax.fori_loop(0, 8, last_rows, 0)

    def last_dot(n, carry):
        cols = pl.ds(pl.multiple_of(n * 256, 256), 256)
        rows = buf[HID, :, :, :, :, cols].reshape(2048, 256)
        acc[:, cols] = jnp.dot(last_w[...], rows, **DOT)
        return carry

    lax.fori_loop(0, WIDTH // 256, last_dot, 0)
    share(COT, 3)
    for t in range(3):
        core_copy(COT, t).wait_recv()
    add_first(0, 5, False)
    share(COT, 4)
    for t in range(3, 5):
        core_copy(COT, t).wait_recv()
    add_first(5, 3, True)

    for k in range(9):
        boot_copy(k).wait_send()
    for array in range(2):
        for part in range(3):
            for way in range(2):
                for t in range(4):
                    z_copy(array, way, t, part).wait_send()
        for t in range(1, 5):
            for dim in range(2):
                for k in range(4):
                    ring_copy(array, dim, t, k).wait_send()
        for t in range(5):
            core_copy(array, t).wait_send()
    for k in range(2):
        stat_core(k).wait_send()
    for axis in range(3):
        for k in range(1, counts[axis]):
            stat_axis(axis, k).wait_send()
    for n in range(WIDTH // 256):
        cols = pl.ds(n * 256, 256)
        pltpu.make_async_copy(out_v.at[:, cols], out.at[:, cols], local_sem.at[2 + n]).wait()


def body(activations, token_ids, embed_table):
    bf16, f32, dma = jnp.bfloat16, jnp.float32, pltpu.SemaphoreType.DMA
    grad = pl.pallas_call(
        kernel,
        out_shape=jax.ShapeDtypeStruct((ROWS, WIDTH), bf16),
        in_specs=[
            pl.BlockSpec(memory_space=pl.ANY),
            pl.BlockSpec(memory_space=pltpu.VMEM),
            pl.BlockSpec(memory_space=pl.ANY),
        ],
        out_specs=pl.BlockSpec(memory_space=pl.ANY),
        scratch_shapes=[
            pltpu.VMEM((2, 8, 2, 8, 16, WIDTH), bf16),
            pltpu.VMEM((ROWS, WIDTH), bf16),
            pltpu.VMEM((8, ROWS, 256), f32),
            pltpu.VMEM((ROWS, 2048), bf16),
            pltpu.VMEM((ROWS, 2048), bf16),
            pltpu.VMEM((ROWS, WIDTH), f32),
            pltpu.VMEM((ROWS, WIDTH), bf16),
            pltpu.VMEM((2, 2, 8, 128), f32),
            pltpu.VMEM((2, 8, 128), f32),
            pltpu.VMEM((4, 2, 8, 128), f32),
            pltpu.VMEM((X - 1, 2, 8, 128), f32),
            pltpu.VMEM((Y - 1, 2, 8, 128), f32),
            pltpu.VMEM((Z - 1, 2, 8, 128), f32),
            pltpu.VMEM((2, 2, 8, 128), f32),
            dma((10,)),
            dma((9,)), dma((9,)),
            dma((2, 2, 4, 3)), dma((2, 2, 4, 3)),
            dma((2, 2, 4, 4)), dma((2, 2, 4, 4)),
            dma((2, 5)), dma((2, 5)),
            dma((15,)), dma((15,)),
        ],
        compiler_params=pltpu.CompilerParams(
            collective_id=0, has_side_effects=True, vmem_limit_bytes=48 << 20
        ),
    )(activations.reshape(8, 16, WIDTH), token_ids, embed_table)
    return grad.reshape(1, 1, ROWS, WIDTH)


def solution(mesh):
    in_specs = (P("section", "dp", None), P(), P(("dp", "vocab"), None))
    out_specs = P(("dp", "vocab"), "section", None, None)
    return jax.shard_map(body, mesh=mesh, in_specs=in_specs, out_specs=out_specs, check_vma=False)
```

time: 162 us -> 83.1 us (0.51)
  Pallas kernels: 0 us -> 78.5 us
  waiting for transfers between devices: 74.2 us -> 0 us
  blocking collectives: 47.1 us -> 0 us
  matrix products: 18.6 us -> 0 us
  between operations: 13.5 us -> 0.01 us
  starting transfers between devices: 3.78 us -> 0 us
  local copies, waits for them, and re-layouts: 1.39 us -> 4.32 us
  other arithmetic: 2.85 us -> 0 us
    pallas_call x0 -> x1, Pallas kernels: none -> 78.5 us  [body(): pl.pallas_call(kernel, out_shape=jax.ShapeDtypeStruct((ROWS, WIDTH), bf16...]
    all_gather x2 -> x0, waiting for transfers between devices: 62.6 us -> none  [the longest x1 60.1 us: spread_rows(): lax.all_gather(row_tuple[1], DP, axis=0, tiled=True)]
    all_gather x5 -> x0, blocking collectives: 47.1 us -> none  [collected_together(): both, at, found = (lax.all_gather(jnp.concatenate(lines), axis), 0, {})]
    dot_general x3 -> x0, matrix products: 18.6 us -> none  [the longest x1 6.89 us: body(): lax.dot_general(last_part, hid_all, (((0,), (0,)), ((), ())), preferred_e...]
    ppermute x1 -> x0, waiting for transfers between devices: 10.9 us -> none  [from_partner(): return lax.ppermute(block, axis, route)]
    ppermute x1 -> x0, starting transfers between devices: 3.73 us -> none  [from_partner(): return lax.ppermute(block, axis, route)]
    unnamed x8 -> x7, local copies, waits for them, and re-layouts: 1.34 us -> 4.32 us
    select_n x1 -> x0, other arithmetic: 2.1 us -> none  [body(): hid_rows = jnp.where(section_index == 0, partner, own_rows)]
  transfers between devices with their start and end apart: 3 -> 0, of which waited for: 3 -> 0; matrix products, arithmetic and copies ran while one was open for 4% -> 0% of each run, Pallas kernels for 0% -> 0%
where the time goes in v1:
time: 83.1 us; the launch traced here: 82.9 us
  Pallas kernels  78.5 us (94%)
  local copies, waits for them, and re-layouts  4.32 us (5%)
    pallas_call x1, Pallas kernels, body(): pl.pallas_call(kernel, out_shape=jax.ShapeDtypeStruct((ROWS, WIDTH), bf16...  78.5 us
    unnamed x7, local copies, waits for them, and re-layouts  4.32 us

profile of v1, /device:TPU:1, one launch (start us, length us, event | category | flops | bytes accessed | tf_op | source)
XLA Modules:
  0.0 82.9 jit_solution(2788478910337755142)
XLA Ops:
  0.0 0.0 copy-start
  0.0 1.6 %copy-done = bf16[512,2048]{1,0:T(8,128)(2,1)S(1)} copy-done((bf16[512,2048]{1,0:T(8,128)(2,1)S(1)}, bf16[512,2048]{1,0:T(8,128)(2,1)}, u32[]{:S(2)}) %copy-start) | copy-done | bytes 2097176
  1.6 0.0 copy-start.1
  1.6 1.0 %copy-done.1 = bf16[1,128,2048]{2,1,0:T(8,128)(2,1)S(1)} copy-done((bf16[1,128,2048]{2,1,0:T(8,128)(2,1)S(1)}, bf16[1,128,2048]{2,1,0:T(8,128)(2,1)}, u32[]{:S(2)}) %copy-start.1) | copy-done | bytes 524312
  2.6 0.0 copy-start.2
  2.6 0.7 copy-done.2
  3.4 78.5 %shard_map.37 = bf16[256,2048]{1,0:T(8,128)(2,1)S(1)} custom-call(bf16[8,16,2048]{2,1,0:T(8,128)(2,1)S(1)} %bitcast.3, s32[2,2048]{1,0:T(2,128)S(1)} %copy-done.2, bf16[512,2048]{1,0:T(8,128)(2,1)S(1)} %copy-done), custom_call_target="tpu_custom_call" | custom-call | tf_op jit(solution)/shard_map/pallas_call | solution.py:378
  81.9 1.0 %copy.5 = bf16[1,1,256,2048]{3,2,1,0:T(8,128)(2,1)} copy(bf16[1,1,256,2048]{3,2,1,0:T(8,128)(2,1)S(1)} %bitcast.2) | data formatting | bytes 2097152
Async XLA Ops:
  0.0 1.6 %copy-start = (bf16[512,2048]{1,0:T(8,128)(2,1)S(1)}, bf16[512,2048]{1,0:T(8,128)(2,1)}, u32[]{:S(2)}) copy-start(bf16[512,2048]{1,0:T(8,128)(2,1)} %table.1) | copy-start | bytes 6291460
  1.6 1.0 %copy-start.1 = (bf16[1,128,2048]{2,1,0:T(8,128)(2,1)S(1)}, bf16[1,128,2048]{2,1,0:T(8,128)(2,1)}, u32[]{:S(2)}) copy-start(bf16[1,128,2048]{2,1,0:T(8,128)(2,1)} %param.3) | copy-start | bytes 1572868
  2.6 0.7 copy-start.2

commit v2 on v1

--- a/solution.py
+++ b/solution.py
@@ -12,6 +12,7 @@
 WIDTH = 2048
 CUT_X, CUT_Y = 1024, 1664
 COLUMNS = ((0, CUT_X), (CUT_X, CUT_Y - CUT_X), (CUT_Y, WIDTH - CUT_Y))
+TILE = 512
 ROWS = 256
 DOT = dict(preferred_element_type=jnp.float32)
 
@@ -27,9 +28,9 @@
 
 
 def kernel(
-    act, ids, table, out,
-    buf, tab, scores, last_w, first_w, acc, out_v,
-    own_stat, core_stat, sent_stat, x_stat, y_stat, z_stat, fin_stat,
+    act, ids_hbm, table, out,
+    buf, ids, tab, scores, last_w, first_w, acc, out_v,
+    own_stat, core_stat, sent_stat, plane_stat, z_stat, fin_stat,
     local_sem, boot_s, boot_r, z_s, z_r, ring_s, ring_r, core_s, core_r, stat_s, stat_r,
 ):
     s = lax.axis_index("section")
@@ -46,9 +47,13 @@
     def x_dev(k):
         return {"vocab": yl * 4 + lax.rem(x + k + X, X)}
 
+    def plane_dev(kx, ky):
+        to = lax.rem(y + ky + Y, Y)
+        over = lax.rem(x + kx + X, X)
+        return {"section": lax.div(to, 2), "vocab": lax.rem(to, 2) * 4 + over}
+
     def y_dev(k):
-        to = lax.rem(y + k + Y, Y)
-        return {"section": lax.div(to, 2), "vocab": lax.rem(to, 2) * 4 + x}
+        return plane_dev(0, k)
 
     core_dev = {"dp": z * 2 + 1 - c}
     cross_dev = {"section": 1 - s, "vocab": (1 - yl) * 4 + x}
@@ -63,10 +68,11 @@
     load_own.start()
     load_table = pltpu.make_async_copy(table.at[pl.ds(s * ROWS, ROWS)], tab, local_sem.at[1])
     load_table.start()
+    load_ids = pltpu.make_async_copy(ids_hbm, ids, local_sem.at[2])
+    load_ids.start()
 
     barrier = pltpu.get_barrier_semaphore()
-    peers = [z_dev(k) for k in range(1, Z)] + [x_dev(k) for k in range(1, X)]
-    peers += [y_dev(k) for k in range(1, Y)] + [core_dev]
+    peers = [core_dev] + [dev(k) for dev in (x_dev, y_dev, z_dev) for k in (1, -1)]
     for peer in peers:
         pl.semaphore_signal(barrier, inc=1, device_id=peer, device_id_type=MESH)
 
@@ -167,37 +173,41 @@
         core_copy(HID, t).wait_recv()
         first, count = SLOTS[t]
 
-        def one(slot, carry):
-            rows = buf[HID, slot].reshape(256, WIDTH)
-            block = lax.dot_general(tab[...], rows, (((1,), (1,)), ((), ())), **DOT)
-            scores[slot] = block
-            peak = jnp.max(block, axis=0, keepdims=True)
-            total = jnp.sum(jnp.exp(block - peak), axis=0, keepdims=True)
-            chip = chip_of(slot)
+        rows = buf[HID, pl.ds(first, count)].reshape(count * 256, WIDTH)
+        block = lax.dot_general(tab[...], rows, (((1,), (1,)), ((), ())), **DOT)
+        peak = jnp.max(block, axis=0, keepdims=True)
+        total = jnp.sum(jnp.exp(block - peak), axis=0, keepdims=True)
+        for k in range(count):
+            scores[first + k] = block[:, k * 256 : k * 256 + 256]
+            chip = chip_of(first + k)
             for core in range(2):
-                lanes = slice(core * 128, core * 128 + 128)
+                lanes = slice(k * 256 + core * 128, k * 256 + core * 128 + 128)
                 own_stat[core, 0, pl.ds(chip, 1), :] = peak[:, lanes]
                 own_stat[core, 1, pl.ds(chip, 1), :] = total[:, lanes]
+
+    def tile(n):
+        return pl.ds(pl.multiple_of(n * TILE, TILE), TILE)
+
+    def first_dot(first, count, cols):
+        rows = buf[COT, pl.ds(first, count), :, :, :, cols].reshape(count * 256, TILE)
+        return jnp.dot(first_w[:, first * 256 : (first + count) * 256], rows, **DOT)
+
+    def add_first(t):
+        first, count = SLOTS[t]
+        core_copy(COT, t).wait_recv()
+
+        def one(n, carry):
+            cols = tile(n)
+            part = first_dot(first, count, cols)
+            acc[:, cols] = part if t == 0 else acc[:, cols] + part
             return carry
 
-        lax.fori_loop(first, first + count, one, 0)
-
-    def add_first(first, count, finish):
-        def one(n, carry):
-            cols = pl.ds(pl.multiple_of(n * 256, 256), 256)
-            rows = buf[COT, pl.ds(first, count), :, :, :, cols].reshape(count * 256, 256)
-            part = jnp.dot(first_w[:, first * 256 : (first + count) * 256], rows, **DOT)
-            total = acc[:, cols] + part
-            if finish:
-                out_v[:, cols] = total.astype(jnp.bfloat16)
-                pltpu.make_async_copy(
-                    out_v.at[:, cols], out.at[:, cols], local_sem.at[2 + n]
-                ).start()
-            else:
-                acc[:, cols] = total
-            return carry
-
-        lax.fori_loop(0, WIDTH // 256, one, 0)
+        lax.fori_loop(0, WIDTH // TILE, one, 0)
+
+    def store(n):
+        return pltpu.make_async_copy(
+            out_v.at[:, tile(n)], out.at[:, tile(n)], local_sem.at[3 + n]
+        )
 
     def hot(index, slot, core):
         at = pl.multiple_of(chip_of(slot) * 256 + core * 128, 128)
@@ -212,28 +222,53 @@
             return remote(own_stat.at[1 - c], core_stat, stat_s.at[0], stat_r.at[0], core_dev)
         return remote(sent_stat.at[3], fin_stat.at[c], stat_s.at[1], stat_r.at[1], core_dev)
 
-    def stat_axis(axis, k):
-        into, dev, at = ((x_stat, x_dev, 2), (y_stat, y_dev, 5), (z_stat, z_dev, 8))[axis]
-        at = at + k - 1
-        return remote(sent_stat.at[axis], into.at[k - 1], stat_s.at[at], stat_r.at[at], dev(k))
-
-    counts = (X, Y, Z)
-
-    def stat_send(axis, pairs):
+    def stat_plane(k):
+        dev = plane_dev(k % X, k // X)
+        return remote(
+            sent_stat.at[1], plane_stat.at[k - 1], stat_s.at[1 + k], stat_r.at[1 + k], dev
+        )
+
+    def stat_z(k):
+        return remote(
+            sent_stat.at[2], z_stat.at[k - 1], stat_s.at[16 + k], stat_r.at[16 + k], z_dev(k)
+        )
+
+    def stat_send(stage, pairs):
         peak, total = merge(pairs)
-        sent_stat[axis, 0] = peak
-        sent_stat[axis, 1] = total
-        if axis < 3:
-            for k in range(1, counts[axis]):
-                stat_axis(axis, k).start()
-
-    def stat_take(axis):
-        into = (x_stat, y_stat, z_stat)[axis]
-        pairs = [(sent_stat[axis, 0], sent_stat[axis, 1])]
-        for k in range(1, counts[axis]):
-            stat_axis(axis, k).wait_recv()
-            pairs.append((into[k - 1, 0], into[k - 1, 1]))
-        return pairs
+        sent_stat[stage, 0] = peak
+        sent_stat[stage, 1] = total
+
+    def stat_plane_send():
+        stat_core(0).wait_recv()
+        mine = own_stat[pl.ds(c, 1)]
+        stat_send(1, [(mine[0, 0], mine[0, 1]), (core_stat[0], core_stat[1])])
+        for k in range(1, X * Y):
+            stat_plane(k).start()
+
+    def stat_z_send():
+        pairs = [(sent_stat[1, 0], sent_stat[1, 1])]
+        for k in range(1, X * Y):
+            stat_plane(k).wait_recv()
+            pairs.append((plane_stat[k - 1, 0], plane_stat[k - 1, 1]))
+        stat_send(2, pairs)
+        for k in range(1, Z):
+            stat_z(k).start()
+
+    def stat_fin_send():
+        pairs = [(sent_stat[2, 0], sent_stat[2, 1])]
+        for k in range(1, Z):
+            stat_z(k).wait_recv()
+            pairs.append((z_stat[k - 1, 0], z_stat[k - 1, 1]))
+        stat_send(3, pairs)
+        stat_core(1).start()
+        fin_stat[pl.ds(c, 1)] = sent_stat[pl.ds(3, 1)]
+
+    def share_own(array):
+        @pl.when(s != array)
+        def _():
+            for k in range(3, 9):
+                boot_copy(k).wait_recv()
+            core_copy(array, 0).start()
 
     load_own.wait()
     pl.semaphore_wait(barrier, len(peers))
@@ -257,43 +292,32 @@
             first_w[:, lanes_of(slot, core)] = hot(0, slot, core).astype(jnp.bfloat16)
         return carry
 
+    load_ids.wait()
     lax.fori_loop(0, 8, first_rows, 0)
     load_table.wait()
 
     step_quarters(HID, 1)
     step_whole(HID, 1)
-
-    @pl.when(s == COT)
-    def _():
-        for k in range(3, 9):
-            boot_copy(k).wait_recv()
-        core_copy(HID, 0).start()
-
     step_quarters(HID, 2)
     pass_on(HID, 1)
     step_whole(HID, 2)
     step_quarters(HID, 3)
     pass_on(HID, 2)
     step_whole(HID, 3)
+    share_own(HID)
     share(HID, 1)
+    start(COT)
     score(0)
-    start(COT)
-
-    @pl.when(s == HID)
-    def _():
-        for k in range(3, 9):
-            boot_copy(k).wait_recv()
-        core_copy(COT, 0).start()
-
     step_quarters(HID, 4)
     pass_on(HID, 3)
     step_whole(HID, 4)
     share(HID, 2)
+    share_own(COT)
     score(1)
     pass_on(HID, 4)
     share(HID, 3)
+    step_quarters(COT, 1)
     score(2)
-    step_quarters(COT, 1)
     step_whole(COT, 1)
     share(HID, 4)
     score(3)
@@ -301,24 +325,22 @@
     stat_core(0).start()
     step_quarters(COT, 2)
     pass_on(COT, 1)
-    stat_core(0).wait_recv()
-    mine = own_stat[pl.ds(c, 1)]
-    stat_send(0, [(mine[0, 0], mine[0, 1]), (core_stat[0], core_stat[1])])
+    stat_plane_send()
     step_whole(COT, 2)
-    stat_send(1, stat_take(0))
+    add_first(0)
     step_quarters(COT, 3)
     pass_on(COT, 2)
-    stat_send(2, stat_take(1))
+    share(COT, 1)
+    stat_z_send()
     step_whole(COT, 3)
-    share(COT, 1)
-    stat_send(3, stat_take(2))
-    stat_core(1).start()
-    fin_stat[pl.ds(c, 1)] = sent_stat[pl.ds(3, 1)]
     step_quarters(COT, 4)
     pass_on(COT, 3)
+    add_first(1)
+    stat_fin_send()
     step_whole(COT, 4)
     share(COT, 2)
     pass_on(COT, 4)
+    share(COT, 3)
     stat_core(1).wait_recv()
 
     def last_rows(slot, carry):
@@ -334,21 +356,27 @@
 
     lax.fori_loop(0, 8, last_rows, 0)
 
+    add_first(2)
+
     def last_dot(n, carry):
-        cols = pl.ds(pl.multiple_of(n * 256, 256), 256)
-        rows = buf[HID, :, :, :, :, cols].reshape(2048, 256)
-        acc[:, cols] = jnp.dot(last_w[...], rows, **DOT)
+        cols = tile(n)
+        rows = buf[HID, :, :, :, :, cols].reshape(2048, TILE)
+        acc[:, cols] = acc[:, cols] + jnp.dot(last_w[...], rows, **DOT)
         return carry
 
-    lax.fori_loop(0, WIDTH // 256, last_dot, 0)
-    share(COT, 3)
-    for t in range(3):
-        core_copy(COT, t).wait_recv()
-    add_first(0, 5, False)
+    lax.fori_loop(0, WIDTH // TILE, last_dot, 0)
     share(COT, 4)
     for t in range(3, 5):
         core_copy(COT, t).wait_recv()
-    add_first(5, 3, True)
+
+    def finish(n, carry):
+        cols = tile(n)
+        total = acc[:, cols] + first_dot(5, 3, cols)
+        out_v[:, cols] = total.astype(jnp.bfloat16)
+        store(n).start()
+        return carry
+
+    lax.fori_loop(0, WIDTH // TILE, finish, 0)
 
     for k in range(9):
         boot_copy(k).wait_send()
@@ -365,12 +393,12 @@
             core_copy(array, t).wait_send()
     for k in range(2):
         stat_core(k).wait_send()
-    for axis in range(3):
-        for k in range(1, counts[axis]):
-            stat_axis(axis, k).wait_send()
-    for n in range(WIDTH // 256):
-        cols = pl.ds(n * 256, 256)
-        pltpu.make_async_copy(out_v.at[:, cols], out.at[:, cols], local_sem.at[2 + n]).wait()
+    for k in range(1, X * Y):
+        stat_plane(k).wait_send()
+    for k in range(1, Z):
+        stat_z(k).wait_send()
+    for n in range(WIDTH // TILE):
+        store(n).wait()
 
 
 def body(activations, token_ids, embed_table):
@@ -379,13 +407,14 @@
         kernel,
         out_shape=jax.ShapeDtypeStruct((ROWS, WIDTH), bf16),
         in_specs=[
-            pl.BlockSpec(memory_space=pl.ANY),
-            pl.BlockSpec(memory_space=pltpu.VMEM),
-            pl.BlockSpec(memory_space=pl.ANY),
+            pl.BlockSpec(memory_space=pltpu.HBM),
+            pl.BlockSpec(memory_space=pltpu.HBM),
+            pl.BlockSpec(memory_space=pltpu.HBM),
         ],
-        out_specs=pl.BlockSpec(memory_space=pl.ANY),
+        out_specs=pl.BlockSpec(memory_space=pltpu.HBM),
         scratch_shapes=[
             pltpu.VMEM((2, 8, 2, 8, 16, WIDTH), bf16),
+            pltpu.VMEM((2, 2048), jnp.int32),
             pltpu.VMEM((ROWS, WIDTH), bf16),
             pltpu.VMEM((8, ROWS, 256), f32),
             pltpu.VMEM((ROWS, 2048), bf16),
@@ -395,19 +424,18 @@
             pltpu.VMEM((2, 2, 8, 128), f32),
             pltpu.VMEM((2, 8, 128), f32),
             pltpu.VMEM((4, 2, 8, 128), f32),
-            pltpu.VMEM((X - 1, 2, 8, 128), f32),
-            pltpu.VMEM((Y - 1, 2, 8, 128), f32),
+            pltpu.VMEM((X * Y - 1, 2, 8, 128), f32),
             pltpu.VMEM((Z - 1, 2, 8, 128), f32),
             pltpu.VMEM((2, 2, 8, 128), f32),
-            dma((10,)),
+            dma((3 + WIDTH // TILE,)),
             dma((9,)), dma((9,)),
             dma((2, 2, 4, 3)), dma((2, 2, 4, 3)),
             dma((2, 2, 4, 4)), dma((2, 2, 4, 4)),
             dma((2, 5)), dma((2, 5)),
-            dma((15,)), dma((15,)),
+            dma((24,)), dma((24,)),
         ],
         compiler_params=pltpu.CompilerParams(
-            collective_id=0, has_side_effects=True, vmem_limit_bytes=48 << 20
+            collective_id=0, has_side_effects=True, vmem_limit_bytes=67_043_328
         ),
     )(activations.reshape(8, 16, WIDTH), token_ids, embed_table)
     return grad.reshape(1, 1, ROWS, WIDTH)

time: 83.1 us -> 72.7 us (0.87)
  Pallas kernels: 78.5 us -> 70.2 us
  local copies, waits for them, and re-layouts: 4.32 us -> 2.3 us
    pallas_call x1, Pallas kernels: 78.5 us -> 70.2 us  [body(): pl.pallas_call(kernel, out_shape=jax.ShapeDtypeStruct((ROWS, WIDTH), bf16...]
    unnamed x7 -> x1, local copies, waits for them, and re-layouts: 4.32 us -> 2.3 us
where the time goes in v2:
time: 72.7 us; the launch traced here: 72.5 us
  Pallas kernels  70.2 us (97%)
  local copies, waits for them, and re-layouts  2.3 us (3%)
    pallas_call x1, Pallas kernels, body(): pl.pallas_call(kernel, out_shape=jax.ShapeDtypeStruct((ROWS, WIDTH), bf16...  70.2 us
    unnamed x1, local copies, waits for them, and re-layouts  2.3 us

profile of v2, /device:TPU:1, one launch (start us, length us, event | category | flops | bytes accessed | tf_op | source)
XLA Modules:
  0.0 72.5 jit_solution(8812745017096402176)
XLA Ops:
  0.0 70.2 %shard_map.37 = bf16[256,2048]{1,0:T(8,128)(2,1)} custom-call(bf16[8,16,2048]{2,1,0:T(8,128)(2,1)} %bitcast.3, s32[2,2048]{1,0:T(2,128)} %ids_hbm.1, bf16[512,2048]{1,0:T(8,128)(2,1)} %table.1), custom_call_target="tpu_custom_call" | custom-call | tf_op jit(solution)/shard_map/pallas_call | solution.py:406
  70.2 2.3 %copy.5 = bf16[1,1,256,2048]{3,2,1,0:T(8,128)(2,1)} copy(bf16[1,1,256,2048]{3,2,1,0:T(8,128)(2,1)} %bitcast.2) | data formatting | bytes 2097152
